TPU v7x, 32 devices: a whole 2x2x4 slice. The times are simulated.
32 devices in a mesh: groups: 2 (over y), ctx: 4 (over z), tp: 4 (over x, core).
Axes of the slice: x: 2, y: 2, z: 4, core: 2. Of those that a mesh axis runs over, the one named last changes fastest.
Arguments:
- query_matrix: bfloat16 [1024, 8192], P(('groups', 'ctx'), 'tp'), parts along dimension 0, may hold values from -20 to 20
- key_matrix: bfloat16 [1024, 1024], P(('groups', 'ctx'), 'tp'), parts along dimension 0, may hold values from -20 to 20
- value_matrix: bfloat16 [1024, 1024], P(('groups', 'ctx'), 'tp'), parts along dimension 0, may hold values from -6 to 6
- doc_ids: int32 [1024], P('groups'), parts along dimension 0, may hold values from 0 to 5, never falling along the last dimension, each value on 1 to 256 neighbouring positions
- out_weight: bfloat16 [8192, 4096], P('tp', 'ctx'), may hold values from -0.0625 to 0.0625
Outputs:
- projected: bfloat16 [1024, 4096], P(('groups', 'ctx'), 'tp'), parts along dimension 0
There are 2 independent parts, one for each index of `groups`. A program takes and returns all parts, laid end to end along the dimension named above; an argument that names none is the same for every part. Nothing has to cross between parts.
Inputs may be any that keep to these rules, and one draw needn't show every extreme that they name: `doc_ids`: non-decreasing along the sequence; each document holds 1 to 256 tokens, one exactly 256.
All inputs are finite; a program needn't handle non-finite values.
Results may differ from a plain program's by a relative error of at most 0.015.
Values may be sent and summed in bfloat16 or wider, within the bound.
A program may use at most 64 MiB of HBM per device.

v0:
```python
import math

import jax
import jax.numpy as jnp
from jax import lax
from jax.sharding import PartitionSpec as P

HEAD_SIZE = 128


rope_base = 1000000.0


def rotary_tables(rows, token_positions, heads):
    half_dim = HEAD_SIZE // 2
    frequency = jnp.power(
        jnp.float32(rope_base), -jnp.arange(half_dim, dtype=jnp.float32) * (2.0 / HEAD_SIZE)
    )
    angles = token_positions.astype(jnp.float32)[:, None] * frequency[None, :]
    cosine = jnp.cos(angles)[:, None, :]
    sine = jnp.sin(angles)[:, None, :]
    values = rows.astype(jnp.float32).reshape(rows.shape[0], heads, HEAD_SIZE)
    first = values[..., :half_dim]
    second = values[..., half_dim:]
    turned = jnp.concatenate([first * cosine - second * sine, second * cosine + first * sine], -1)
    return turned.reshape(rows.shape[0], heads * HEAD_SIZE).astype(jnp.bfloat16)


def on_device(query_matrix, key_matrix, value_matrix, doc_ids, out_weight):
    ctx_index = lax.axis_index("ctx")
    tok_rows = query_matrix.shape[0]
    query_heads = query_matrix.shape[1] // HEAD_SIZE
    key_heads = key_matrix.shape[1] // HEAD_SIZE
    group_width = query_heads // key_heads
    inverse_root = HEAD_SIZE ** (-0.5)
    local_rows = jnp.arange(tok_rows, dtype=jnp.int32)
    given_pos = ctx_index * tok_rows + local_rows
    query_matrix_rot = rotary_tables(query_matrix, given_pos, query_heads)
    keys_here = rotary_tables(key_matrix, given_pos, key_heads)
    query_doc = jnp.take(doc_ids, given_pos, axis=0)
    query_four = query_matrix_rot.reshape(tok_rows, key_heads, group_width, HEAD_SIZE)

    def attend(state, block):
        key_block, value_block, doc_block, pos_block = block
        row_max, totals, accum = state
        scores = (
            jnp.einsum("qkgd,skd->kgqs", query_four, key_block, preferred_element_type=jnp.float32)
            * inverse_root
        )
        allowed = (
            (query_doc[:, None] == doc_block[None, :]) & (pos_block[None, :] <= given_pos[:, None])
        )[None, None]
        new_max = jnp.maximum(row_max, jnp.max(jnp.where(allowed, scores, -1e30), -1))
        weights = jnp.where(allowed, jnp.exp(scores - new_max[..., None]), 0.0)
        factor = jnp.exp(row_max - new_max)
        totals = totals * factor + jnp.sum(weights, -1)
        accum = accum * jnp.transpose(factor, (2, 0, 1))[..., None] + jnp.einsum(
            "kgqs,skd->qkgd",
            weights.astype(jnp.bfloat16),
            value_block,
            preferred_element_type=jnp.float32,
        )
        return (new_max, totals, accum)

    start_state = (
        jnp.full((key_heads, group_width, tok_rows), -1e30, jnp.float32),
        jnp.zeros((key_heads, group_width, tok_rows), jnp.float32),
        jnp.zeros((tok_rows, key_heads, group_width, HEAD_SIZE), jnp.float32),
    )
    key_piece = lax.all_gather(keys_here, "ctx", axis=0, tiled=True)
    value_piece = lax.all_gather(value_matrix, "ctx", axis=0, tiled=True)
    count = key_piece.shape[0]
    block_rows = math.gcd(count, 512)
    block_count = count // block_rows
    positions = jnp.arange(count, dtype=jnp.int32)
    blocks = (
        key_piece.reshape(block_count, block_rows, key_heads, HEAD_SIZE),
        value_piece.reshape(block_count, block_rows, key_heads, HEAD_SIZE),
        jnp.take(doc_ids, positions, axis=0).reshape(block_count, block_rows),
        positions.reshape(block_count, block_rows),
    )

    def step_block(inner_state, block):
        return (attend(inner_state, block), None)

    final_state, unused_out = lax.scan(step_block, start_state, blocks)
    row_max, totals, accum = final_state
    attention = (
        (accum / jnp.transpose(totals, (2, 0, 1))[..., None])
        .reshape(tok_rows, query_heads * HEAD_SIZE)
        .astype(jnp.bfloat16)
    )
    terms = jnp.dot(
        attention,
        lax.all_gather(out_weight, "ctx", axis=1, tiled=True),
        preferred_element_type=jnp.float32,
    )
    return lax.psum_scatter(terms.astype(jnp.bfloat16), "tp", scatter_dimension=1, tiled=True)


def solution(mesh):
    in_specs = (
        P(("groups", "ctx"), "tp"),
        P(("groups", "ctx"), "tp"),
        P(("groups", "ctx"), "tp"),
        P("groups"),
        P("tp", "ctx"),
    )
    out_specs = P(("groups", "ctx"), "tp")
    return jax.shard_map(
        on_device, mesh=mesh, in_specs=in_specs, out_specs=out_specs, check_vma=False
    )
```

profile of v0, /device:TPU:3, one launch (start us, length us, event | category | flops | bytes accessed | tf_op | source)
XLA Modules:
  0.0 340.0 jit_solution(13007268321086336774)
XLA Ops:
  6.5 0.0 copy-start
  6.5 0.0 copy-start.1
  6.5 0.0 copy-start.2
  6.5 0.0 all-gather.2.cloned.1.call-start
  6.5 0.7 all-gather.2.cloned.1.call-update
  7.3 0.0 copy-start.3
  7.3 0.0 reduce-scatter.2.cloned.1.call-start
  7.4 0.2 multiply_cosine_fusion
  7.6 0.1 copy.22
  7.6 0.1 copy.24
  7.8 0.0 copy-done.1
  7.8 0.1 convert_bitcast_fusion
  7.9 0.2 copy.36
  8.1 0.0 copy-done.2
  8.1 0.1 copy.33
  8.2 0.0 copy-done
  8.2 1.3 gather_fusion
  9.5 3.5 %gather_fusion.1 = s32[512]{0:T(512)S(1)} fusion(s32[512]{0:T(512)S(1)} %copy-done, s32[1024]{0:T(1024)S(1)} %pad_clamp_fusion), kind=kCustom, calls=%fused_computation.1 | custom fusion | bytes 6144 | tf_op jit(solution)/shard_map/jit(_take)/gather | solution.py:79
  13.0 0.0 copy-done.3
  13.0 12.5 %all_gather.10 = bf16[512,256]{1,0:T(8,128)(2,1)S(1)} all-gather(bf16[128,256]{1,0:T(8,128)(2,1)S(1)} %copy-done.3), channel_id=1, replica_groups=mesh['groups'=2,'ctx'=4,'tp'=4] {'ctx'}, dimensions={0}, use_global_device_ids=true | all-gather | bytes 327680 | tf_op jit(solution)/shard_map/all_gather | solution.py:71
  25.5 0.1 copy.26
  25.7 30.1 %all_gather.9 = bf16[512,256]{0,1:T(8,128)(2,1)S(1)} all-gather(bf16[128,256]{0,1:T(8,128)(2,1)S(1)} %bitcast.61), channel_id=1, replica_groups=mesh['groups'=2,'ctx'=4,'tp'=4] {'ctx'}, dimensions={0}, use_global_device_ids=true | all-gather | bytes 327680 | tf_op jit(solution)/shard_map/all_gather | solution.py:70
  55.8 0.3 fusion.25
  56.1 0.7 subtract_convert_fusion
  56.8 0.3 pad_maximum_fusion
  57.1 0.1 fusion.19
  57.3 0.8 fusion
  58.1 0.9 fusion.3
  59.0 1.0 divide_convert_fusion
  60.1 242.0 %all-gather.2.cloned.1.call-done = bf16[2048,4096]{1,0:T(8,128)(2,1)} async-done(((bf16[2048,1024]{1,0:T(8,128)(2,1)}), bf16[2048,4096]{1,0:T(8,128)(2,1)}) %all-gather.2.cloned.1.call-update) | async-done | bytes 16777232 | tf_op jit(solution)/shard_map/all_gather | solution.py:95
  302.0 9.1 %convolution_convert_fusion = bf16[128,4096]{1,0:T(8,128)(2,1)} fusion(bf16[128,2048]{0,1:T(8,128)(2,1)S(1)} %bitcast.59, bf16[2048,4096]{1,0:T(8,128)(2,1)} %all-gather.2.cloned.1.call-done), kind=kOutput, calls=%fused_computation.2 | convolution fusion | flops 2148007936 | bytes 18350080 | tf_op jit(solution)/shard_map/dot_general | solution.py:93
  311.2 0.0 reduce-scatter.2.cloned.1.call-update
  311.2 22.0 %reduce-scatter.2.cloned.1.call-done = bf16[128,1024]{1,0:T(8,128)(2,1)} async-done(((bf16[128,4096]{1,0:T(8,128)(2,1)}), bf16[128,1024]{1,0:T(8,128)(2,1)}) %reduce-scatter.2.cloned.1.call-update) | async-done | bytes 262160 | tf_op jit(solution)/shard_map/reduce_scatter | solution.py:98
  (12 shorter events, 0.1 us)
Async XLA Ops:
  6.5 1.7 copy-start
  6.5 1.2 copy-start.1
  6.5 1.5 copy-start.2
  6.5 295.5 %all-gather.2.cloned.1.call-start = ((), (), s32[]{:S(2)}) async-start(), calls=%async_computation.1 | async-start | bytes 20971520 | tf_op jit(solution)/shard_map/all_gather | solution.py:95
  7.3 5.8 %copy-start.3 = (bf16[128,256]{1,0:T(8,128)(2,1)S(1)}, bf16[128,256]{1,0:T(8,128)(2,1)}, u32[]{:S(2)}) copy-start(bf16[128,256]{1,0:T(8,128)(2,1)} %param.7) | copy-start | bytes 196612
  7.3 325.9 %reduce-scatter.2.cloned.1.call-start = ((), (), s32[]{:S(2)}) async-start(), calls=%async_computation.2 | async-start | bytes 1310720 | tf_op jit(solution)/shard_map/reduce_scatter | solution.py:98
Sparse Core Ops, SparseCore 0:
  8.9 293.0 all-gather.1
  311.3 21.8 reduce-scatter.1
where the time goes:
time: 343 us; the launch traced here: 340 us
  waiting for transfers between devices  265 us (77%)
  blocking collectives  42.5 us (12%)
  between operations  13.6 us (4%)
  matrix products  11 us (3%)
  local copies, waits for them, and re-layouts  5.75 us (2%)
    all_gather x1, waiting for transfers between devices, on_device(): lax.all_gather(out_weight, 'ctx', axis=1, tiled=True)  242 us
    all_gather x1, blocking collectives, on_device(): key_piece = lax.all_gather(keys_here, 'ctx', axis=0, tiled=True)  30.1 us
    reduce_scatter x1, waiting for transfers between devices, on_device(): lax.psum_scatter(terms.astype(jnp.bfloat16), 'tp', scatter_dimension=1, t...  22 us
    all_gather x1, blocking collectives, on_device(): value_piece = lax.all_gather(value_matrix, 'ctx', axis=0, tiled=True)  12.5 us
    dot_general x1, matrix products, on_device(): jnp.dot(attention, lax.all_gather(out_weight, 'ctx', axis=1, tiled=True),...  9.13 us
  transfers between devices with their start and end apart: 2, of which 2 were waited for; matrix products, arithmetic and copies ran while one was open for 3% of the time, Pallas kernels for 0%

commit v1 on v0

--- a/solution.py
+++ b/solution.py
@@ -1,9 +1,15 @@
+import functools
 import math
 
 import jax
 import jax.numpy as jnp
+import numpy as np
 from jax import lax
+from jax.experimental import pallas as pl
+from jax.experimental.pallas import tpu as pltpu
 from jax.sharding import PartitionSpec as P
+
+MESH = pl.DeviceIdType.MESH
 
 HEAD_SIZE = 128
 
@@ -98,6 +104,347 @@
     return lax.psum_scatter(terms.astype(jnp.bfloat16), "tp", scatter_dimension=1, tiled=True)
 
 
+def fused_kernel(
+    n, back, query_ref, key_ref, value_ref, doc_ref, table_ref, weight_ref, out_ref,
+    query_in, key_in, table, docs, weight, rotated, bias, kv, gathered, total_lo, total_hi,
+    partial, quarters, summed, landed,
+    load_sem, weight_sem, kv_send, kv_recv, up_send, down_send, chunk_recv,
+    quarter_send, quarter_recv, result_send, result_recv, store_sem,
+):
+    ctx = lax.axis_index("ctx")
+    tp = lax.axis_index("tp")
+    rows = query_ref.shape[0]
+    kv_heads = key_ref.shape[1] // HEAD_SIZE
+    query_heads = query_ref.shape[1] // HEAD_SIZE
+    group_width = query_heads // kv_heads
+    chunks = gathered.shape[1]
+    chunk_width = gathered.shape[3]
+    chunk_heads = chunk_width // HEAD_SIZE
+    quarter = partial.shape[3]
+    last = n - 1
+
+    def remote(src, dst, send, recv, to_ctx, to_tp):
+        return pltpu.make_async_remote_copy(
+            src_ref=src, dst_ref=dst, send_sem=send, recv_sem=recv,
+            device_id={"ctx": to_ctx, "tp": to_tp}, device_id_type=MESH,
+        )
+
+    barrier = pltpu.get_barrier_semaphore()
+    for step in range(1, n * n):
+        pl.semaphore_signal(
+            barrier, inc=1,
+            device_id={"ctx": lax.rem(ctx + step // n, n), "tp": lax.rem(tp + step % n, n)},
+            device_id_type=MESH,
+        )
+
+    first_row = pl.multiple_of(ctx * rows, rows)
+    loads = [
+        pltpu.make_async_copy(key_ref, key_in, load_sem.at[0]),
+        pltpu.make_async_copy(table_ref.at[:, pl.ds(first_row, rows)], table, load_sem.at[1]),
+        pltpu.make_async_copy(doc_ref, docs, load_sem.at[2]),
+        pltpu.make_async_copy(query_ref, query_in, load_sem.at[3]),
+    ]
+    value_loads = [
+        pltpu.make_async_copy(
+            value_ref.at[:, pl.ds(head * HEAD_SIZE, HEAD_SIZE)], kv.at[back, head, 1], load_sem.at[4 + head]
+        )
+        for head in range(kv_heads)
+    ]
+    weight_loads = [
+        pltpu.make_async_copy(
+            weight_ref.at[pl.ds(chunk * chunk_width, chunk_width)], weight.at[chunk], weight_sem.at[chunk]
+        )
+        for chunk in range(chunks)
+    ]
+    for load in loads + value_loads + weight_loads:
+        load.start()
+
+    def turn(values):
+        values = values.astype(jnp.float32)
+        return (values * table[0] + pltpu.roll(values, HEAD_SIZE // 2, 1) * table[1]).astype(jnp.bfloat16)
+
+    loads[0].wait()
+    loads[1].wait()
+    for head in range(kv_heads):
+        kv[back, head, 0] = turn(key_in[:, head * HEAD_SIZE : (head + 1) * HEAD_SIZE])
+    for load in value_loads:
+        load.wait()
+
+    for slot in range(back):
+        @pl.when(ctx < back - slot)
+        def _():
+            kv[slot] = jnp.zeros(kv.shape[1:], kv.dtype)
+
+    pl.semaphore_wait(barrier, n * n - 1)
+
+    def kv_copy(slot, head):
+        return remote(
+            kv.at[slot, head], kv.at[slot - 1, head], kv_send.at[slot, head], kv_recv.at[slot - 1, head],
+            lax.rem(ctx + 1, n), tp,
+        )
+
+    def kv_sends(slot):
+        return (ctx < last) & (ctx >= back - slot)
+
+    @pl.when(ctx < last)
+    def _():
+        for head in range(kv_heads):
+            kv_copy(back, head).start()
+
+    loads[2].wait()
+    own_docs = jnp.broadcast_to(docs[pl.ds(ctx, 1), :], (rows, rows)).astype(jnp.float32).T
+    row_index = lax.broadcasted_iota(jnp.int32, (rows, rows), 0)
+    column_index = lax.broadcasted_iota(jnp.int32, (rows, rows), 1)
+    for slot in range(back + 1):
+        block = ctx - back + slot
+        their_docs = docs[pl.ds(lax.max(block, 0), 1), :].astype(jnp.float32)
+        allowed = (own_docs == their_docs) & (block * rows + column_index <= ctx * rows + row_index) & (block >= 0)
+        bias[slot] = jnp.where(allowed, 0.0, -1e30)
+
+    loads[3].wait()
+    for head in range(query_heads):
+        rotated[head] = turn(query_in[:, head * HEAD_SIZE : (head + 1) * HEAD_SIZE])
+
+    for slot in range(back - 1, 0, -1):
+        for head in range(kv_heads):
+            @pl.when(ctx >= back - slot)
+            def _():
+                kv_copy(slot + 1, head).wait_recv()
+
+            @pl.when(kv_sends(slot))
+            def _():
+                kv_copy(slot, head).start()
+
+    def up_copy(block, chunk):
+        here = gathered.at[block, chunk]
+        return remote(here, here, up_send.at[block, chunk], chunk_recv.at[block, chunk], lax.rem(ctx + 1, n), tp)
+
+    def down_copy(block, chunk):
+        here = gathered.at[block, chunk]
+        return remote(here, here, down_send.at[block, chunk], chunk_recv.at[block, chunk], lax.rem(ctx + last, n), tp)
+
+    scale = HEAD_SIZE ** (-0.5) * math.log2(math.e)
+    contract = (((1,), (1,)), ((), ()))
+    for head in range(query_heads):
+        kv_head = head // group_width
+        if head % group_width == 0:
+            @pl.when(ctx >= back)
+            def _():
+                kv_copy(1, kv_head).wait_recv()
+
+        scores = [
+            lax.dot_general(rotated[head], kv[slot, kv_head, 0], contract, preferred_element_type=jnp.float32) * scale
+            + bias[slot]
+            for slot in range(back + 1)
+        ]
+        row_max = functools.reduce(jnp.maximum, scores).max(-1, keepdims=True)
+        weights = [jnp.exp2(score - row_max) for score in scores]
+        totals = sum(weights).sum(-1, keepdims=True)
+        mixed = sum(
+            jnp.dot(weights[slot].astype(jnp.bfloat16), kv[slot, kv_head, 1], preferred_element_type=jnp.float32)
+            for slot in range(back + 1)
+        )
+        chunk, place = head // chunk_heads, head % chunk_heads
+        gathered[ctx, chunk, :, place * HEAD_SIZE : (place + 1) * HEAD_SIZE] = (mixed / totals).astype(jnp.bfloat16)
+        if place == chunk_heads - 1:
+            @pl.when(ctx < last)
+            def _():
+                up_copy(ctx, chunk).start()
+
+            @pl.when(ctx > 0)
+            def _():
+                down_copy(ctx, chunk).start()
+
+    def quarter_copy(block, hop):
+        to = lax.rem(tp + hop, n)
+        return remote(
+            partial.at[block, to], quarters.at[block, hop], quarter_send.at[block, hop], quarter_recv.at[block, hop],
+            ctx, to,
+        )
+
+    def project(block, chunk, total):
+        for hop in list(range(1, n)) + [0]:
+            part = lax.rem(tp + hop, n)
+            columns = pl.ds(pl.multiple_of(part * quarter, quarter), quarter)
+            product = jnp.dot(
+                gathered[block, chunk], weight[chunk, :, columns], preferred_element_type=jnp.float32
+            )
+            if chunk > 0:
+                product = product + total[hop]
+            if chunk < chunks - 1:
+                total[hop] = product
+            else:
+                partial[block, part] = product.astype(jnp.bfloat16)
+                if hop:
+                    quarter_copy(block, hop).start()
+
+    def result_copy(block):
+        return remote(
+            summed.at[block], landed.at[tp], result_send.at[block], result_recv.at[tp], block, ctx
+        )
+
+    def finish(block):
+        value = partial[block, tp].astype(jnp.float32)
+        for hop in range(1, n):
+            quarter_copy(block, hop).wait_recv()
+            value = value + quarters[block, hop].astype(jnp.float32)
+        value = value.astype(jnp.bfloat16)
+        mine = (block == ctx) & (tp == ctx)
+
+        @pl.when(mine)
+        def _():
+            landed[tp] = value
+
+        @pl.when(jnp.logical_not(mine))
+        def _():
+            summed[block] = value
+            result_copy(block).start()
+
+    for load in weight_loads:
+        load.wait()
+    for chunk in range(chunks):
+        project(ctx, chunk, total_lo)
+
+    def finish_pair(step):
+        @pl.when(ctx - step >= 0)
+        def _():
+            finish(lax.max(ctx - step, 0))
+
+        @pl.when((ctx + step <= last) & (step > 0))
+        def _():
+            finish(lax.min(ctx + step, last))
+
+    def gather_step(step, carry):
+        low, high = lax.max(ctx - step, 0), lax.min(ctx + step, last)
+        has_low, has_high = ctx - step >= 0, ctx + step <= last
+        for chunk in range(chunks):
+            @pl.when(has_low)
+            def _():
+                up_copy(low, chunk).wait_recv()
+
+                @pl.when(ctx < last)
+                def _():
+                    up_copy(low, chunk).start()
+
+            @pl.when(has_high)
+            def _():
+                down_copy(high, chunk).wait_recv()
+
+                @pl.when(ctx > 0)
+                def _():
+                    down_copy(high, chunk).start()
+
+            @pl.when(has_low)
+            def _():
+                project(low, chunk, total_lo)
+
+            @pl.when(has_high)
+            def _():
+                project(high, chunk, total_hi)
+
+        finish_pair(step - 1)
+        return carry
+
+    lax.fori_loop(1, n, gather_step, 0)
+    finish_pair(last)
+
+    for part in range(n):
+        @pl.when(jnp.logical_not((tp == ctx) & (tp == part)))
+        def _():
+            remote(
+                summed.at[0], landed.at[part], result_send.at[0], result_recv.at[part], ctx, part
+            ).wait_recv()
+
+        pltpu.make_async_copy(
+            landed.at[part], out_ref.at[:, pl.ds(part * quarter, quarter)], store_sem.at[part]
+        ).start()
+
+    for slot in range(1, back + 1):
+        for head in range(kv_heads):
+            @pl.when(kv_sends(slot))
+            def _():
+                kv_copy(slot, head).wait_send()
+
+    def drain(block, carry):
+        for chunk in range(chunks):
+            @pl.when((block <= ctx) & (ctx < last))
+            def _():
+                up_copy(block, chunk).wait_send()
+
+            @pl.when((block >= ctx) & (ctx > 0))
+            def _():
+                down_copy(block, chunk).wait_send()
+
+        for hop in range(1, n):
+            quarter_copy(block, hop).wait_send()
+
+        @pl.when(jnp.logical_not((block == ctx) & (tp == ctx)))
+        def _():
+            result_copy(block).wait_send()
+
+        return carry
+
+    lax.fori_loop(0, n, drain, 0)
+    for part in range(n):
+        pltpu.make_async_copy(
+            landed.at[part], out_ref.at[:, pl.ds(part * quarter, quarter)], store_sem.at[part]
+        ).wait()
+
+
+def fused(n, query_matrix, key_matrix, value_matrix, doc_ids, out_weight):
+    rows, query_width = query_matrix.shape
+    query_heads, kv_heads = query_width // HEAD_SIZE, key_matrix.shape[1] // HEAD_SIZE
+    features = out_weight.shape[1]
+    tokens = doc_ids.shape[0]
+    back = -(-(tokens // 2 - 1) // rows)
+    chunks = 4
+    chunk_width = query_width // chunks
+    quarter = features // n
+    half = HEAD_SIZE // 2
+    frequency = np.power(np.float32(rope_base), -np.arange(half, dtype=np.float32) * np.float32(2.0 / HEAD_SIZE))
+    angles = np.arange(tokens, dtype=np.float32)[:, None] * frequency[None, :]
+    cosine, sine = np.cos(angles), np.sin(angles)
+    table = np.stack([np.concatenate([cosine, cosine], 1), np.concatenate([-sine, sine], 1)]).astype(np.float32)
+    any_space = pl.BlockSpec(memory_space=pl.ANY)
+    bf16, f32, dma = jnp.bfloat16, jnp.float32, pltpu.SemaphoreType.DMA
+    return pl.pallas_call(
+        functools.partial(fused_kernel, n, back),
+        out_shape=jax.ShapeDtypeStruct((rows, features), bf16),
+        in_specs=[any_space] * 6,
+        out_specs=any_space,
+        scratch_shapes=[
+            pltpu.VMEM((rows, query_width), bf16),
+            pltpu.VMEM((rows, kv_heads * HEAD_SIZE), bf16),
+            pltpu.VMEM((2, rows, HEAD_SIZE), f32),
+            pltpu.VMEM((tokens // rows, rows), jnp.int32),
+            pltpu.VMEM((chunks, chunk_width, features), bf16),
+            pltpu.VMEM((query_heads, rows, HEAD_SIZE), bf16),
+            pltpu.VMEM((back + 1, rows, rows), f32),
+            pltpu.VMEM((back + 1, kv_heads, 2, rows, HEAD_SIZE), bf16),
+            pltpu.VMEM((n, chunks, rows, chunk_width), bf16),
+            pltpu.VMEM((n, rows, quarter), f32),
+            pltpu.VMEM((n, rows, quarter), f32),
+            pltpu.VMEM((n, n, rows, quarter), bf16),
+            pltpu.VMEM((n, n, rows, quarter), bf16),
+            pltpu.VMEM((n, rows, quarter), bf16),
+            pltpu.VMEM((n, rows, quarter), bf16),
+            dma((4 + kv_heads,)),
+            dma((chunks,)),
+            dma((back + 1, kv_heads)),
+            dma((back + 1, kv_heads)),
+            dma((n, chunks)),
+            dma((n, chunks)),
+            dma((n, chunks)),
+            dma((n, n)),
+            dma((n, n)),
+            dma((n,)),
+            dma((n,)),
+            dma((n,)),
+        ],
+        compiler_params=pltpu.CompilerParams(collective_id=0, has_side_effects=True),
+    )(query_matrix, key_matrix, value_matrix, doc_ids.reshape(tokens // rows, rows), jnp.asarray(table), out_weight)
+
+
 def solution(mesh):
     in_specs = (
         P(("groups", "ctx"), "tp"),
@@ -107,6 +454,8 @@
         P("tp", "ctx"),
     )
     out_specs = P(("groups", "ctx"), "tp")
+    n = mesh.shape["ctx"]
+    body = functools.partial(fused, n) if n == mesh.shape["tp"] else on_device
     return jax.shard_map(
-        on_device, mesh=mesh, in_specs=in_specs, out_specs=out_specs, check_vma=False
-    )
+        body, mesh=mesh, in_specs=in_specs, out_specs=out_specs, check_vma=False
+    )

time: 343 us -> 60.3 us (0.18)
  waiting for transfers between devices: 265 us -> 0 us
  Pallas kernels: 0 us -> 58.4 us
  blocking collectives: 42.5 us -> 0 us
  between operations: 13.6 us -> 0.01 us
  matrix products: 11 us -> 0 us
  local copies, waits for them, and re-layouts: 5.75 us -> 1.67 us
    all_gather x1 -> x0, waiting for transfers between devices: 242 us -> none  [on_device(): lax.all_gather(out_weight, 'ctx', axis=1, tiled=True)]
    pallas_call x0 -> x1, Pallas kernels: none -> 58.4 us  [fused(): pl.pallas_call(functools.partial(fused_kernel, n, back), out_shape=jax.Sh...]
    all_gather x2 -> x0, blocking collectives: 42.5 us -> none  [the longest x1 30.1 us: on_device(): key_piece = lax.all_gather(keys_here, 'ctx', axis=0, tiled=True)]
    reduce_scatter x1 -> x0, waiting for transfers between devices: 22 us -> none  [on_device(): lax.psum_scatter(terms.astype(jnp.bfloat16), 'tp', scatter_dimension=1, t...]
    dot_general x3 -> x0, matrix products: 11 us -> none  [the longest x1 9.13 us: on_device(): jnp.dot(attention, lax.all_gather(out_weight, 'ctx', axis=1, tiled=True),...]
    gather x2 -> x0, local copies, waits for them, and re-layouts: 4.78 us -> none  [the longest x1 3.51 us: on_device(): jnp.take(doc_ids, positions, axis=0).reshape(block_count, block_rows)]
  transfers between devices with their start and end apart: 2 -> 0, of which waited for: 2 -> 0; matrix products, arithmetic and copies ran while one was open for 3% -> 0% of each run, Pallas kernels for 0% -> 0%
where the time goes in v1:
time: 60.3 us; the launch traced here: 60.1 us
  Pallas kernels  58.4 us (97%)
  local copies, waits for them, and re-layouts  1.67 us (3%)
    pallas_call x1, Pallas kernels, fused(): pl.pallas_call(functools.partial(fused_kernel, n, back), out_shape=jax.Sh...  58.4 us
    unnamed x1, local copies, waits for them, and re-layouts  1.67 us

profile of v1, /device:TPU:3, one launch (start us, length us, event | category | flops | bytes accessed | tf_op | source)
XLA Modules:
  0.0 60.1 jit_solution(17149103454918903040)
XLA Ops:
  0.0 58.4 %shard_map.64 = bf16[128,1024]{1,0:T(8,128)(2,1)} custom-call(bf16[128,2048]{1,0:T(8,128)(2,1)} %query_ref.1, bf16[128,256]{1,0:T(8,128)(2,1)} %key_ref.1, bf16[128,256]{1,0:T(8,128)(2,1)} %value_ref.1, s32[4,128]{1,0:T(4,128)} %bitcast.1, f32[2,512,128]{2,1,0:T(8,128)} %constant.2.clone.table_ref, bf16[2048,1024]{1,0:T(8,128)(2,1)} %weight_ref.1), custom_call_target="tpu_custom_call" | custom-call | tf_op jit(solution)/shard_map/pallas_call | solution.py:410
  58.4 1.7 %copy.8 = bf16[128,1024]{1,0:T(8,128)(2,1)} copy(bf16[128,1024]{1,0:T(8,128)(2,1)} %shard_map.64) | data formatting | bytes 524288
